TPU v7x, 32 devices: a whole 2x2x4 slice. The times are simulated.
32 devices in a mesh: wide: 16 (over z, y, core), narrow: 2 (over x).
Axes of the slice: x: 2, y: 2, z: 4, core: 2. Of those that a mesh axis runs over, the one named last changes fastest.
Arguments:
- hidden_in: bfloat16 [16384, 1024], P(('wide', 'narrow')), may hold values from -6 to 6
- segment_ids: int32 [32, 512], P(('wide', 'narrow')), may hold values from 0 to 7, never falling along the last dimension, each value on 1 to 256 neighbouring positions
- expert_ids: int32 [16384, 8], P(('wide', 'narrow')), may hold values from 0 to 15, all different within a row; in each aligned block of 512 rows (0 to 511, 512 to 1023, ...) at most 512 rows name the same one
- attn_gain: float32 [1024], replicated, may hold values from 0.5 to 1.5
- w_query: bfloat16 [1024, 1024], replicated, may hold values from -0.1875 to 0.1875
- w_key: bfloat16 [1024, 512], replicated, may hold values from -0.1875 to 0.1875
- w_value: bfloat16 [1024, 512], replicated, may hold values from -0.1875 to 0.1875
- w_out: bfloat16 [1024, 1024], replicated, may hold values from -0.75 to 0.75
- ffn_gain: float32 [1024], replicated, may hold values from 0.5 to 1.5
- router: bfloat16 [1024, 16], replicated, may hold values from -0.1875 to 0.1875
- w_gate: bfloat16 [16, 1024, 512], P('wide', None, 'narrow'), may hold values from -0.1875 to 0.1875
- w_up: bfloat16 [16, 1024, 512], P('wide', None, 'narrow'), may hold values from -0.1875 to 0.1875
- w_down: bfloat16 [16, 512, 1024], P('wide', 'narrow'), may hold values from -0.75 to 0.75
- grad_out: bfloat16 [16384, 1024], P(('wide', 'narrow')), may hold values from -6 to 6
Outputs:
- hidden_out: bfloat16 [16384, 1024], P(('wide', 'narrow'))
- grad_in: bfloat16 [16384, 1024], P(('wide', 'narrow'))
- grad_attn_gain: float32 [1024], replicated
- grad_query: float32 [1024, 1024], replicated
- grad_key: float32 [1024, 512], replicated
- grad_value: float32 [1024, 512], replicated
- grad_out_proj: float32 [1024, 1024], replicated
- grad_ffn_gain: float32 [1024], replicated
- grad_router: float32 [1024, 16], replicated
- grad_gate: float32 [16, 1024, 512], P('wide', None, 'narrow')
- grad_up: float32 [16, 1024, 512], P('wide', None, 'narrow')
- grad_down: float32 [16, 512, 1024], P('wide', 'narrow')
Inputs may be any that keep to these rules, and one draw needn't show every extreme that they name: `segment_ids`: each packed row has 8 documents numbered in order from 0, each of 1 to half of 512 tokens, one of exactly half of 512. `expert_ids`: each token names 8 different experts. Among the 512 tokens of one packed row no expert is named more than 512 times, and in every draw some row names some expert exactly 512 times.
All inputs are finite; a program needn't handle non-finite values.
Results may differ from a plain program's by a relative error of at most 0.015.
Values may be sent and summed in bfloat16 or wider, within the bound.
A program may use at most 320 MiB of HBM per device.

v0:
```python
import jax
import jax.numpy as jnp
from jax import lax
from jax.sharding import PartitionSpec as P

HD = 64
EPSILON = 1e-05


def norm_scale(values):
    return lax.rsqrt(jnp.mean(values * values, axis=-1, keepdims=True) + EPSILON)


def norm_back(values, inv_rms, gain_vector, grad_rows):
    weighted = grad_rows * gain_vector
    inner = jnp.mean(weighted * values, axis=-1, keepdims=True)
    value_grad = inv_rms * weighted - values * (inv_rms * inv_rms * inv_rms) * inner
    return (value_grad, jnp.sum(grad_rows * values * inv_rms, axis=0))


def rope_tables(length, head_dim):
    half_size = head_dim // 2
    freqs = 10000.0 ** (-(jnp.arange(half_size, dtype=jnp.float32) * 2.0) / head_dim)
    angles = jnp.arange(length, dtype=jnp.float32)[:, None] * freqs[None, :]
    return (jnp.cos(angles), jnp.sin(angles))


def rotate(values, cosine_table, sine_table, direction):
    half_size = values.shape[-1] // 2
    first_half = values[..., :half_size]
    second_half = values[..., half_size:]
    cosine_part = cosine_table[:, None, :]
    sine_part = sine_table[:, None, :] * direction
    return jnp.concatenate(
        [
            first_half * cosine_part - second_half * sine_part,
            second_half * cosine_part + first_half * sine_part,
        ],
        axis=-1,
    )


def attention_probs(grouped, key_rows, allowed, head_dim):
    scores = jnp.einsum(
        "qngd,knd->ngqk", grouped, key_rows, preferred_element_type=jnp.float32
    ) * head_dim ** (-0.5)
    return jnp.where(allowed, scores, -1e30)


def on_device(
    hidden_in,
    segment_ids,
    expert_ids,
    attn_gain,
    w_query,
    w_key,
    w_value,
    w_out,
    ffn_gain,
    router,
    w_gate,
    w_up,
    w_down,
    grad_out,
):
    f32 = jnp.float32
    bf16 = jnp.bfloat16
    length, model_width = hidden_in.shape
    head_dim = HD
    head_count = w_query.shape[1] // head_dim
    kv_count = w_key.shape[1] // head_dim
    group_size = head_count // kv_count
    experts = router.shape[1]
    top_count = expert_ids.shape[1]
    slot_count = min(length, 2 * length * top_count // experts)
    inputs = hidden_in.astype(f32)
    scale_one = norm_scale(inputs)
    normed = (inputs * scale_one * attn_gain).astype(bf16)
    query_pre = jnp.dot(normed, w_query, preferred_element_type=f32)
    key_pre = jnp.dot(normed, w_key, preferred_element_type=f32)
    value_pre = jnp.dot(normed, w_value, preferred_element_type=f32)
    cosine_table, sine_table = rope_tables(length, head_dim)
    query_rows = rotate(
        query_pre.reshape(length, head_count, head_dim), cosine_table, sine_table, 1.0
    ).astype(bf16)
    key_rows = rotate(
        key_pre.reshape(length, kv_count, head_dim), cosine_table, sine_table, 1.0
    ).astype(bf16)
    value_rows = value_pre.astype(bf16).reshape(length, kv_count, head_dim)
    grouped = query_rows.reshape(length, kv_count, group_size, head_dim)
    segments = segment_ids[0]
    places = jnp.arange(length, dtype=jnp.int32)
    allowed = (segments[:, None] == segments[None, :]) & (places[:, None] >= places[None, :])
    scores = attention_probs(grouped, key_rows, allowed, head_dim)
    row_max = jnp.max(scores, axis=-1, keepdims=True)
    log_total = row_max + jnp.log(jnp.sum(jnp.exp(scores - row_max), axis=-1, keepdims=True))
    weights_prob = jnp.exp(scores - log_total)
    attended = jnp.einsum(
        "ngqk,knd->qngd", weights_prob.astype(bf16), value_rows, preferred_element_type=f32
    )
    attended = attended.reshape(length, head_count * head_dim).astype(bf16)
    mixed_rows = inputs + jnp.dot(attended, w_out, preferred_element_type=f32)
    scale_two = norm_scale(mixed_rows)
    ffn_normed = (mixed_rows * scale_two * ffn_gain).astype(bf16)
    logits = jnp.dot(ffn_normed, router, preferred_element_type=f32)
    chosen = jnp.take_along_axis(logits, expert_ids, axis=1)
    gate_probs = jax.nn.softmax(chosen, axis=-1)
    picked = expert_ids[:, :, None] == jnp.arange(experts, dtype=jnp.int32)[None, None, :]
    member = jnp.any(picked, axis=1)
    ranks = jnp.cumsum(member.astype(jnp.int32), axis=0) - 1
    slot_of = jnp.sum(jnp.where(picked, ranks[:, None, :], 0), axis=2)
    flat_slot = (expert_ids * slot_count + slot_of).reshape(-1)
    token_of_copy = jnp.repeat(jnp.arange(length, dtype=jnp.int32), top_count)
    send_index = (
        jnp.full((experts * slot_count,), length, jnp.int32).at[flat_slot].set(token_of_copy)
    )
    padded = jnp.concatenate([ffn_normed, jnp.zeros((1, model_width), bf16)], axis=0)
    outgoing = padded[send_index].reshape(experts, slot_count, model_width)
    incoming = lax.all_to_all(outgoing, "wide", split_axis=0, concat_axis=0, tiled=True)
    rows_in = incoming.reshape(-1, model_width)
    full_gate, full_up, full_down = (
        lax.all_gather(w_gate, "narrow", axis=2, tiled=True),
        lax.all_gather(w_up, "narrow", axis=2, tiled=True),
        lax.all_gather(w_down, "narrow", axis=1, tiled=True),
    )
    gate_act = jnp.dot(rows_in, full_gate[0], preferred_element_type=f32)
    up_act = jnp.dot(rows_in, full_up[0], preferred_element_type=f32)
    hidden_act = (jax.nn.silu(gate_act) * up_act).astype(bf16)
    outputs = jnp.dot(hidden_act, full_down[0], preferred_element_type=f32).astype(bf16)
    returned = lax.all_to_all(
        outputs.reshape(experts, slot_count, model_width),
        "wide",
        split_axis=0,
        concat_axis=0,
        tiled=True,
    )
    gathered = returned.reshape(-1, model_width)[flat_slot].reshape(length, top_count, model_width)
    moe_rows = jnp.sum(gate_probs[:, :, None] * gathered.astype(f32), axis=1)
    hidden_out = (mixed_rows + moe_rows).astype(bf16)
    cotangent = grad_out.astype(f32)
    gate_grads = jnp.einsum("sd,skd->sk", grad_out, gathered, preferred_element_type=f32)
    chosen_grads = gate_probs * (
        gate_grads - jnp.sum(gate_probs * gate_grads, axis=-1, keepdims=True)
    )
    logit_grads = jnp.sum(jnp.where(picked, chosen_grads[:, :, None], 0.0), axis=1).astype(bf16)
    router_grad = jnp.einsum("sd,se->de", ffn_normed, logit_grads, preferred_element_type=f32)
    normed_two_grad = jnp.einsum("se,de->sd", logit_grads, router, preferred_element_type=f32)
    slot_gates = jnp.zeros((experts * slot_count,), f32).at[flat_slot].set(gate_probs.reshape(-1))
    padded_grad = jnp.concatenate([grad_out, jnp.zeros((1, model_width), bf16)], axis=0)
    out_grads = (slot_gates[:, None] * padded_grad[send_index].astype(f32)).astype(bf16)
    grads_in = lax.all_to_all(
        out_grads.reshape(experts, slot_count, model_width),
        "wide",
        split_axis=0,
        concat_axis=0,
        tiled=True,
    )
    grads_in = grads_in.reshape(-1, model_width)
    hidden_grad = jnp.einsum("rd,fd->rf", grads_in, full_down[0], preferred_element_type=f32)
    down_w_grad = jnp.einsum("rf,rd->fd", hidden_act, grads_in, preferred_element_type=f32)
    sigmoid_gate = jax.nn.sigmoid(gate_act)
    gate_grad = (
        hidden_grad * up_act * sigmoid_gate * (1.0 + gate_act * (1.0 - sigmoid_gate))
    ).astype(bf16)
    up_grad = (hidden_grad * gate_act * sigmoid_gate).astype(bf16)
    gate_w_grad = jnp.einsum("rd,rf->df", rows_in, gate_grad, preferred_element_type=f32)
    up_w_grad = jnp.einsum("rd,rf->df", rows_in, up_grad, preferred_element_type=f32)
    copy_grads = (
        jnp.einsum("rf,df->rd", gate_grad, full_gate[0], preferred_element_type=f32)
        + jnp.einsum("rf,df->rd", up_grad, full_up[0], preferred_element_type=f32)
    ).astype(bf16)
    gate_w_grad, up_w_grad, down_w_grad = (
        lax.psum_scatter(
            gate_w_grad[None].astype(jnp.bfloat16), "narrow", scatter_dimension=2, tiled=True
        ).astype(jnp.float32),
        lax.psum_scatter(
            up_w_grad[None].astype(jnp.bfloat16), "narrow", scatter_dimension=2, tiled=True
        ).astype(jnp.float32),
        lax.psum_scatter(
            down_w_grad[None].astype(jnp.bfloat16), "narrow", scatter_dimension=1, tiled=True
        ).astype(jnp.float32),
    )
    copy_back = lax.all_to_all(
        copy_grads.reshape(experts, slot_count, model_width),
        "wide",
        split_axis=0,
        concat_axis=0,
        tiled=True,
    )
    copy_rows_back = copy_back.reshape(-1, model_width)[flat_slot].reshape(
        length, top_count, model_width
    )
    normed_two_grad = normed_two_grad + jnp.sum(copy_rows_back.astype(f32), axis=1)
    mixed_part, ffn_gain_grad = norm_back(mixed_rows, scale_two, ffn_gain, normed_two_grad)
    mixed_grad = cotangent + mixed_part
    branch_grad = mixed_grad.astype(bf16)
    out_w_grad = jnp.einsum("sh,sd->hd", attended, branch_grad, preferred_element_type=f32)
    attended_grad = jnp.einsum("sd,hd->sh", branch_grad, w_out, preferred_element_type=f32).astype(
        bf16
    )
    attended_grad = attended_grad.reshape(length, kv_count, group_size, head_dim)
    scores = attention_probs(grouped, key_rows, allowed, head_dim)
    weights_prob = jnp.exp(scores - log_total)
    value_grad = jnp.einsum(
        "ngqk,qngd->knd", weights_prob.astype(bf16), attended_grad, preferred_element_type=f32
    )
    prob_grad = jnp.einsum("qngd,knd->ngqk", attended_grad, value_rows, preferred_element_type=f32)
    score_grad = (
        weights_prob * (prob_grad - jnp.sum(weights_prob * prob_grad, axis=-1, keepdims=True))
    ).astype(bf16)
    query_grad = jnp.einsum(
        "ngqk,knd->qngd", score_grad, key_rows, preferred_element_type=f32
    ) * head_dim ** (-0.5)
    key_grad = jnp.einsum(
        "ngqk,qngd->knd", score_grad, grouped, preferred_element_type=f32
    ) * head_dim ** (-0.5)
    query_grad = rotate(
        query_grad.reshape(length, head_count, head_dim), cosine_table, sine_table, -1.0
    )
    query_grad = query_grad.reshape(length, -1).astype(bf16)
    key_grad = rotate(key_grad, cosine_table, sine_table, -1.0).reshape(length, -1).astype(bf16)
    value_grad = value_grad.reshape(length, -1).astype(bf16)
    query_w_grad = jnp.einsum("sd,sh->dh", normed, query_grad, preferred_element_type=f32)
    key_w_grad = jnp.einsum("sd,sh->dh", normed, key_grad, preferred_element_type=f32)
    value_w_grad = jnp.einsum("sd,sh->dh", normed, value_grad, preferred_element_type=f32)
    normed_one_grad = (
        jnp.einsum("sh,dh->sd", query_grad, w_query, preferred_element_type=f32)
        + jnp.einsum("sh,dh->sd", key_grad, w_key, preferred_element_type=f32)
        + jnp.einsum("sh,dh->sd", value_grad, w_value, preferred_element_type=f32)
    )
    input_part, attn_gain_grad = norm_back(inputs, scale_one, attn_gain, normed_one_grad)
    grad_in = (mixed_grad + input_part).astype(bf16)
    summed = lax.psum(
        (
            attn_gain_grad,
            query_w_grad,
            key_w_grad,
            value_w_grad,
            out_w_grad,
            ffn_gain_grad,
            router_grad,
        ),
        ("wide", "narrow"),
    )
    return (
        hidden_out,
        grad_in,
        summed[0],
        summed[1],
        summed[2],
        summed[3],
        summed[4],
        summed[5],
        summed[6],
        gate_w_grad,
        up_w_grad,
        down_w_grad,
    )


def solution(mesh):
    return jax.shard_map(
        on_device,
        mesh=mesh,
        in_specs=(
            P(("wide", "narrow"), None),
            P(("wide", "narrow"), None),
            P(("wide", "narrow"), None),
            P(),
            P(),
            P(),
            P(),
            P(),
            P(),
            P(),
            P("wide", None, "narrow"),
            P("wide", None, "narrow"),
            P("wide", "narrow", None),
            P(("wide", "narrow"), None),
        ),
        out_specs=(
            P(("wide", "narrow"), None),
            P(("wide", "narrow"), None),
            P(),
            P(),
            P(),
            P(),
            P(),
            P(),
            P(),
            P("wide", None, "narrow"),
            P("wide", None, "narrow"),
            P("wide", "narrow", None),
        ),
        check_vma=False,
    )
```

profile of v0, /device:TPU:0, one launch (start us, length us, event | category | flops | bytes accessed | tf_op | source)
XLA Modules:
  0.0 2124.6 jit_solution(18212974689426877776)
XLA Ops:
  24.0 8.3 exponential_reduce_fusion
  32.3 8.5 fusion.22
  46.2 15.5 scatter_custom_fusion
  64.7 35.5 %gather_fusion = bf16[8192,1024]{1,0:T(8,128)(2,1)} fusion(bf16[513,1024]{1,0:T(8,128)(2,1)S(1)} %concatenate.31, s32[8192]{0:T(1024)S(1)} %fusion.53), kind=kCustom, calls=%fused_computation | custom fusion | bytes 33587200 | tf_op jit(solution)/shard_map/gather | solution.py:118
  109.9 22.7 %all-gather.4.cloned.1.call-done = bf16[1,1024,512]{2,1,0:T(8,128)(2,1)} async-done(((bf16[1,1024,256]{2,1,0:T(8,128)(2,1)}), bf16[1,1024,512]{2,1,0:T(8,128)(2,1)}) %all-gather.4.cloned.1.call-update) | async-done | bytes 1048592 | tf_op jit(solution)/shard_map/all_gather | solution.py:122
  132.6 271.7 %all-to-all-done = bf16[16,512,1024]{2,1,0:T(8,128)(2,1)} async-done(((bf16[16,512,1024]{2,1,0:T(8,128)(2,1)}), bf16[16,512,1024]{2,1,0:T(8,128)(2,1)}, u32[]{:S(2)}, u32[]{:S(2)}) %all-to-all-start) | async-done | bytes 16777248 | tf_op jit(solution)/shard_map/all_to_all | solution.py:119
  404.3 16.4 fusion.44
  420.8 21.8 %multiply_convert_fusion.2 = (bf16[8192,512]{1,0:T(8,128)(2,1)}, f32[8192,512]{1,0:T(8,128)}) fusion(f32[8192,512]{1,0:T(8,128)} %fusion.44, bf16[8192,1024]{1,0:T(8,128)(2,1)} %bitcast.18, bf16[1,1024,512]{2,1,0:T(8,128)(2,1)} %all-gather.6.cloned.1.call-done), kind=kOutput, calls=%fused_computation.20 | convolution fusion | flops 8615100416 | bytes 59768832 | tf_op jit(solution)/shard_map/dot_general | solution.py:127
  442.6 14.8 convolution_convert_fusion
  457.4 70.6 %all-to-all-start.1 = ((bf16[16,512,1024]{2,1,0:T(8,128)(2,1)}), bf16[16,512,1024]{2,1,0:T(8,128)(2,1)}, u32[]{:S(2)}, u32[]{:S(2)}) async-start(bf16[16,512,1024]{2,1,0:T(8,128)(2,1)} %bitcast.172), calls=%async_computation.1 | async-start | bytes 33554432 | tf_op jit(solution)/shard_map/all_to_all | solution.py:130
  528.7 33.0 %gather_fusion.4 = f32[4096]{0:T(1024)S(1)} fusion(f32[512,16]{0,1:T(8,128)S(1)} %fusion.82, s32[4096]{0:T(1024)S(1)} %reshape.343), kind=kCustom, calls=%fused_computation.4 | custom fusion | bytes 65536 | tf_op jit(solution)/shard_map/jit(take_along_axis)/gather | solution.py:106
  563.3 35.5 %gather_fusion.2 = bf16[8192,1024]{1,0:T(8,128)(2,1)} fusion(bf16[513,1024]{1,0:T(8,128)(2,1)S(1)} %concatenate.32, s32[8192]{0:T(1024)S(1)} %copy-done.42), kind=kCustom, calls=%fused_computation.2 | custom fusion | bytes 33587200 | tf_op jit(solution)/shard_map/gather | solution.py:150
  598.9 225.7 %all-to-all-done.1 = bf16[16,512,1024]{2,1,0:T(8,128)(2,1)} async-done(((bf16[16,512,1024]{2,1,0:T(8,128)(2,1)}), bf16[16,512,1024]{2,1,0:T(8,128)(2,1)}, u32[]{:S(2)}, u32[]{:S(2)}) %all-to-all-start.1) | async-done | bytes 16777248 | tf_op jit(solution)/shard_map/all_to_all | solution.py:130
  824.6 28.9 %gather_fusion.1 = bf16[4096,1024]{1,0:T(8,128)(2,1)} fusion(bf16[8192,1024]{1,0:T(8,128)(2,1)} %bitcast.23, s32[4096]{0:T(1024)S(1)} %broadcast_clamp_fusion), kind=kCustom, calls=%fused_computation.1 | custom fusion | bytes 16793600 | tf_op jit(solution)/shard_map/gather | solution.py:137
  853.5 7.9 fusion.5
  861.9 15.5 scatter_custom_fusion.1
  877.5 9.2 fusion
  886.7 432.1 %all_to_all.20 = bf16[16,512,1024]{2,1,0:T(8,128)(2,1)} all-to-all(bf16[16,512,1024]{2,1,0:T(8,128)(2,1)S(1)} %fusion), channel_id=1, replica_groups=mesh['wide'=16,'narrow'=2] {'wide'}, dimensions={0} | all-to-all | bytes 33554432 | tf_op jit(solution)/shard_map/all_to_all | solution.py:151
  1318.7 28.7 %multiply_convert_fusion = (bf16[8192,512]{1,0:T(8,128)(2,1)}, bf16[8192,512]{1,0:T(8,128)(2,1)}) fusion(f32[8192,512]{1,0:T(8,128)} %fusion.44, f32[8192,512]{1,0:T(8,128)} %get-tuple-element.49, bf16[8192,1024]{1,0:T(8,128)(2,1)} %bitcast.170, bf16[1,512,1024]{2,1,0:T(8,128)(2,1)} %all-gather.8.cloned.1.call-done), kind=kOutput, calls=%fused_computation.17 | convolution fusion | flops 8644460544 | bytes 68157440 | tf_op jit(solution)/shard_map/rd,fd->rf/dot_general | solution.py:159
  1347.4 18.8 fusion.42
  1366.2 23.6 %add_convert_fusion = bf16[8192,1024]{1,0:T(8,128)(2,1)} fusion(f32[8192,1024]{1,0:T(8,128)} %fusion.42, bf16[8192,512]{1,0:T(8,128)(2,1)} %get-tuple-element.25, bf16[1,1024,512]{2,1,0:T(8,128)(2,1)} %all-gather.6.cloned.1.call-done), kind=kOutput, calls=%fused_computation.9 | convolution fusion | flops 8606711808 | bytes 59768832 | tf_op jit(solution)/shard_map/rf,df->rd/dot_general | solution.py:170
  1397.5 9.8 multiply_reduce_fusion
  1407.4 15.6 fusion.27
  1423.1 15.9 fusion.25
  1439.0 15.6 fusion.26
  1454.7 238.4 %all-to-all-done.3 = bf16[16,512,1024]{2,1,0:T(8,128)(2,1)} async-done(((bf16[16,512,1024]{2,1,0:T(8,128)(2,1)}), bf16[16,512,1024]{2,1,0:T(8,128)(2,1)}, u32[]{:S(2)}, u32[]{:S(2)}) %all-to-all-start.3) | async-done | bytes 16777248 | tf_op jit(solution)/shard_map/all_to_all | solution.py:183
  1693.2 29.0 %gather_fusion.3 = bf16[4096,1024]{1,0:T(8,128)(2,1)} fusion(bf16[8192,1024]{1,0:T(8,128)(2,1)} %bitcast.30, s32[4096]{0:T(1024)S(1)} %copy-done.44), kind=kCustom, calls=%fused_computation.3 | custom fusion | bytes 16793600 | tf_op jit(solution)/shard_map/gather | solution.py:190
  1722.2 11.9 convert_reduce_fusion
  1745.3 14.7 fusion.1
  1762.1 11.0 fusion.3
  1817.6 107.0 %all-reduce.2 = (f32[1024]{0:T(1024)}, f32[1024]{0:T(1024)}) all-reduce(f32[1024]{0:T(1024)S(1)} %get-tuple-element.14, f32[1024]{0:T(1024)S(1)} %get-tuple-element.12), channel_id=1, replica_groups=mesh['wide'=16,'narrow'=2] {'wide','narrow'}, use_global_device_ids=true, to_apply=%region_20.21 | all-reduce | flops 2048 | bytes 16384 | tf_op jit(solution)/shard_map/psum | solution.py:233
  1928.4 177.5 %all-reduce.6.cloned.1.call-done = (f32[1024,1024]{1,0:T(8,128)}, f32[1024,512]{1,0:T(8,128)}, f32[1024,512]{1,0:T(8,128)}, f32[1024,1024]{1,0:T(8,128)}, f32[1024,16]{0,1:T(8,128)}) async-done(((f32[1024,1024]{1,0:T(8,128)}, f32[1024,512]{1,0:T(8,128)}, f32[1024,512]{1,0:T(8,128)}, f32[1024,1024]{1,0:T(8,128)}, f32[1024,16]{0,1:T(8,128)}), (f32[1024,1024]{1,0:T(8,128)}, f32[1024,512]{1,0:T(8,128)}, ...) | async-done | bytes 12648464 | tf_op jit(solution)/shard_map/psum | solution.py:233
  (234 shorter events, 117.8 us)
Async XLA Ops:
  7.2 33.7 %copy-start = (bf16[1024,1024]{1,0:T(8,128)(2,1)S(1)}, bf16[1024,1024]{1,0:T(8,128)(2,1)}, u32[]{:S(2)}) copy-start(bf16[1024,1024]{1,0:T(8,128)(2,1)} %param.21) | copy-start | bytes 6291460
  16.5 15.8 copy-start.20
  40.9 21.0 copy-start.54
  44.1 56.1 %copy-start.56 = (f32[512]{0:T(512)}, f32[512]{0:T(512)S(1)}, u32[]{:S(2)}) copy-start(f32[512]{0:T(512)S(1)} %get-tuple-element.40) | copy-start | bytes 6148
  46.0 54.2 %copy-start.48 = (s32[4096,1]{0,1:T(1,128)}, s32[4096,1]{0,1:T(1,128)S(1)}, u32[]{:S(2)}) copy-start(s32[4096,1]{0,1:T(1,128)S(1)} %compare_select_fusion) | copy-start | bytes 49156
  61.8 38.4 %copy-start.41 = (s32[8192]{0:T(1024)}, s32[8192]{0:T(1024)S(1)}, u32[]{:S(2)}) copy-start(s32[8192]{0:T(1024)S(1)} %fusion.53) | copy-start | bytes 98308
  100.2 304.1 %all-to-all-start = ((bf16[16,512,1024]{2,1,0:T(8,128)(2,1)}), bf16[16,512,1024]{2,1,0:T(8,128)(2,1)}, u32[]{:S(2)}, u32[]{:S(2)}) async-start(bf16[16,512,1024]{2,1,0:T(8,128)(2,1)} %bitcast.168), calls=%async_computation | async-start | bytes 33554432 | tf_op jit(solution)/shard_map/all_to_all | solution.py:119
  107.7 24.9 %all-gather.4.cloned.1.call-start = ((), (), s32[]{:S(2)}) async-start(), calls=%async_computation.7 | async-start | bytes 1572864 | tf_op jit(solution)/shard_map/all_gather | solution.py:122
  108.4 312.3 %all-gather.6.cloned.1.call-start = ((), (), s32[]{:S(2)}) async-start(), calls=%async_computation.8 | async-start | bytes 1572864 | tf_op jit(solution)/shard_map/all_gather | solution.py:123
  109.2 333.4 %all-gather.8.cloned.1.call-start = ((), (), s32[]{:S(2)}) async-start(), calls=%async_computation.9 | async-start | bytes 1572864 | tf_op jit(solution)/shard_map/all_gather | solution.py:124
  457.4 70.9 %copy-start.8 = (bf16[512,1024]{1,0:T(8,128)(2,1)S(1)}, bf16[512,1024]{1,0:T(8,128)(2,1)}, u32[]{:S(2)}) copy-start(bf16[512,1024]{1,0:T(8,128)(2,1)} %copy-done.7) | copy-start | bytes 3145732
  457.4 70.9 %copy-start.45 = (bf16[1024,16]{0,1:T(8,128)(2,1)S(1)}, bf16[1024,16]{0,1:T(8,128)(2,1)}, u32[]{:S(2)}) copy-start(bf16[1024,16]{0,1:T(8,128)(2,1)} %param.23) | copy-start | bytes 98308
  457.4 367.2 %all-to-all-start.1 = ((bf16[16,512,1024]{2,1,0:T(8,128)(2,1)}), bf16[16,512,1024]{2,1,0:T(8,128)(2,1)}, u32[]{:S(2)}, u32[]{:S(2)}) async-start(bf16[16,512,1024]{2,1,0:T(8,128)(2,1)} %bitcast.172), calls=%async_computation.1 | async-start | bytes 33554432 | tf_op jit(solution)/shard_map/all_to_all | solution.py:130
  528.7 34.6 %copy-start.42 = (s32[8192]{0:T(1024)S(1)}, s32[8192]{0:T(1024)}, u32[]{:S(2)}) copy-start(s32[8192]{0:T(1024)} %copy-done.41) | copy-start | bytes 98308
  563.3 35.5 %copy-start.49 = (s32[4096,1]{0,1:T(1,128)S(1)}, s32[4096,1]{0,1:T(1,128)}, u32[]{:S(2)}) copy-start(s32[4096,1]{0,1:T(1,128)} %copy-done.48) | copy-start | bytes 49156
  598.9 254.7 %copy-start.43 = (s32[4096]{0:T(1024)}, s32[4096]{0:T(1024)S(1)}, u32[]{:S(2)}) copy-start(s32[4096]{0:T(1024)S(1)} %broadcast_clamp_fusion) | copy-start | bytes 49156
  824.6 28.9 %copy-start.17 = (bf16[512,1024]{1,0:T(8,128)(2,1)S(1)}, bf16[512,1024]{1,0:T(8,128)(2,1)}, u32[]{:S(2)}) copy-start(bf16[512,1024]{1,0:T(8,128)(2,1)} %param.27) | copy-start | bytes 3145732
  1318.7 28.7 %copy-start.62 = (bf16[1,1024,512]{2,1,0:T(8,128)(2,1)S(1)}, bf16[1,1024,512]{2,1,0:T(8,128)(2,1)}, u32[]{:S(2)}) copy-start(bf16[1,1024,512]{2,1,0:T(8,128)(2,1)} %all-gather.4.cloned.1.call-done) | copy-start | bytes 3145732
  1389.8 303.3 %all-to-all-start.3 = ((bf16[16,512,1024]{2,1,0:T(8,128)(2,1)}), bf16[16,512,1024]{2,1,0:T(8,128)(2,1)}, u32[]{:S(2)}, u32[]{:S(2)}) async-start(bf16[16,512,1024]{2,1,0:T(8,128)(2,1)} %bitcast.169), calls=%async_computation.3 | async-start | bytes 33554432 | tf_op jit(solution)/shard_map/all_to_all | solution.py:183
  1396.5 408.3 %reduce-scatter.8.cloned.1.call-start = ((), (), s32[]{:S(2)}) async-start(), calls=%async_computation.12 | async-start | bytes 1572864 | tf_op jit(solution)/shard_map/reduce_scatter | solution.py:179
  1423.0 384.0 %reduce-scatter.4.cloned.1.call-start = ((), (), s32[]{:S(2)}) async-start(), calls=%async_computation.10 | async-start | bytes 1572864 | tf_op jit(solution)/shard_map/reduce_scatter | solution.py:173
  1438.9 254.2 %copy-start.44 = (s32[4096]{0:T(1024)S(1)}, s32[4096]{0:T(1024)}, u32[]{:S(2)}) copy-start(s32[4096]{0:T(1024)} %copy-done.43) | copy-start | bytes 49156
  1439.0 370.1 %reduce-scatter.6.cloned.1.call-start = ((), (), s32[]{:S(2)}) async-start(), calls=%async_computation.11 | async-start | bytes 1572864 | tf_op jit(solution)/shard_map/reduce_scatter | solution.py:176
  1454.7 651.3 %all-reduce.6.cloned.1.call-start = ((), (), s32[]{:S(2)}) async-start(), calls=%async_computation.13 | async-start | bytes 25296896 | tf_op jit(solution)/shard_map/psum | solution.py:233
  1722.2 11.9 copy-start.46
  1722.2 11.9 copy-start.55
  1722.2 11.9 copy-start.57
  1745.3 14.7 slice-start
  1745.3 14.7 slice-start.1
  1745.3 15.6 slice-start.2
  1745.3 16.8 slice-start.3
  1815.0 109.5 %copy-start.59 = (f32[512]{0:T(512)S(1)}, f32[512]{0:T(512)}, u32[]{:S(2)}) copy-start(f32[512]{0:T(512)} %get-tuple-element.37) | copy-start | bytes 6148
  (45 other events, 219.7 us)
Sparse Core Ops, SparseCore 0:
  110.1 22.4 all-gather.3
  134.1 21.2 all-gather.5
  157.0 21.2 all-gather.7
  1423.1 21.6 reduce-scatter.7
  1446.9 20.3 reduce-scatter.3
  1469.4 20.3 reduce-scatter.5
  1804.9 301.0 all-reduce.5
where the time goes:
time: 2130 us; the launch traced here: 2120 us
  waiting for transfers between devices  938 us (44%)
  blocking collectives  539 us (25%)
  matrix products  260 us (12%)
  local copies, waits for them, and re-layouts  215 us (10%)
  starting transfers between devices  85 us (4%)
  other arithmetic  71.7 us (3%)
    all_to_all x1, blocking collectives, on_device(): lax.all_to_all(out_grads.reshape(experts, slot_count, model_width), 'wide...  432 us
    all_to_all x1, waiting for transfers between devices, on_device(): lax.all_to_all(outgoing, 'wide', split_axis=0, concat_axis=0, tiled=True)  272 us
    all_to_all x1, waiting for transfers between devices, on_device(): lax.all_to_all(copy_grads.reshape(experts, slot_count, model_width), 'wid...  238 us
    all_to_all x1, waiting for transfers between devices, on_device(): lax.all_to_all(outputs.reshape(experts, slot_count, model_width), 'wide',...  226 us
    psum x1, waiting for transfers between devices, on_device(): lax.psum((attn_gain_grad, query_w_grad, key_w_grad, value_w_grad, out_w_g...  178 us
    psum x1, blocking collectives, on_device(): lax.psum((attn_gain_grad, query_w_grad, key_w_grad, value_w_grad, out_w_g...  107 us
    all_to_all x1, starting transfers between devices, on_device(): lax.all_to_all(outputs.reshape(experts, slot_count, model_width), 'wide',...  70.6 us
  transfers between devices with their start and end apart: 10, of which 5 were waited for; matrix products, arithmetic and copies ran while one was open for 14% of the time, Pallas kernels for 0%

commit v1 on v0

--- a/solution.py
+++ b/solution.py
@@ -5,6 +5,30 @@
 
 HD = 64
 EPSILON = 1e-05
+
+
+def keep_up_bench(xs, in_dim, block_here):
+    z, out_arr = (xs.shape[:in_dim], xs.shape[in_dim + 1 :])
+    return jnp.moveaxis(xs.reshape(*z, block_here, -1, *out_arr), in_dim, 0)
+
+
+def produce_series_all_up(panel, dim_at):
+    then = list(panel.shape[1:])
+    then[dim_at] *= panel.shape[0]
+    return jnp.moveaxis(panel, 0, dim_at).reshape(then)
+
+
+def _proceed_stages_all(field_in, ax_name, vector, q_in):
+    upper, y = (lax.axis_size(ax_name), lax.axis_index(ax_name))
+    x_next = keep_up_bench(field_in, vector, upper)
+    views = [x_next[y]]
+    for jj in [*range(1, upper)]:
+        seen_now = x_next[y ^ jj]
+        views.append(
+            lax.ppermute(seen_now, axis_name=ax_name, perm=[(i0, i0 ^ jj) for i0 in range(upper)])
+        )
+    x_next = jnp.stack(views)[y ^ jnp.arange(upper)]
+    return produce_series_all_up(x_next, q_in)
 
 
 def norm_scale(values):
@@ -180,12 +204,8 @@
             down_w_grad[None].astype(jnp.bfloat16), "narrow", scatter_dimension=1, tiled=True
         ).astype(jnp.float32),
     )
-    copy_back = lax.all_to_all(
-        copy_grads.reshape(experts, slot_count, model_width),
-        "wide",
-        split_axis=0,
-        concat_axis=0,
-        tiled=True,
+    copy_back = _proceed_stages_all(
+        copy_grads.reshape(experts, slot_count, model_width), "wide", 0, 0
     )
     copy_rows_back = copy_back.reshape(-1, model_width)[flat_slot].reshape(
         length, top_count, model_width

time: 2130 us -> 2220 us (1.042)
  blocking collectives: 539 us -> 108 us
  waiting for transfers between devices: 938 us -> 1250 us
  starting transfers between devices: 85 us -> 228 us
  local copies, waits for them, and re-layouts: 215 us -> 263 us
    all_to_all x1 -> x0, blocking collectives: 432 us -> none  [on_device(): lax.all_to_all(out_grads.reshape(experts, slot_count, model_width), 'wide...]
    ppermute x0 -> x15, waiting for transfers between devices: none -> 273 us  [_proceed_stages_all(): lax.ppermute(seen_now, axis_name=ax_name, perm=[(i0, i0 ^ jj) for i0 in r...]
    ppermute x0 -> x15, starting transfers between devices: none -> 79.1 us  [_proceed_stages_all(): lax.ppermute(seen_now, axis_name=ax_name, perm=[(i0, i0 ^ jj) for i0 in r...]
    all_to_all x1, starting transfers between devices: 6.7 us -> 70.4 us  [on_device(): lax.all_to_all(out_grads.reshape(experts, slot_count, model_width), 'wide...]
    all_to_all x1, waiting for transfers between devices: 238 us -> 285 us  [on_device(): lax.all_to_all(out_grads.reshape(experts, slot_count, model_width), 'wide...]
  transfers between devices with their start and end apart: 10 -> 25, of which waited for: 5 -> 12; matrix products, arithmetic and copies ran while one was open for 14% -> 18% of each run, Pallas kernels for 0% -> 0%
where the time goes in v1:
time: 2220 us; the launch traced here: 2210 us
  waiting for transfers between devices  1250 us (56%)
  local copies, waits for them, and re-layouts  263 us (12%)
  matrix products  263 us (12%)
  starting transfers between devices  228 us (10%)
  blocking collectives  108 us (5%)
  other arithmetic  82.9 us (4%)
    all_to_all x1, waiting for transfers between devices, on_device(): lax.all_to_all(out_grads.reshape(experts, slot_count, model_width), 'wide...  285 us
    ppermute x15, waiting for transfers between devices, _proceed_stages_all(): lax.ppermute(seen_now, axis_name=ax_name, perm=[(i0, i0 ^ jj) for i0 in r...  273 us
    all_to_all x1, waiting for transfers between devices, on_device(): lax.all_to_all(outgoing, 'wide', split_axis=0, concat_axis=0, tiled=True)  272 us
    all_to_all x1, waiting for transfers between devices, on_device(): lax.all_to_all(outputs.reshape(experts, slot_count, model_width), 'wide',...  225 us
    psum x1, waiting for transfers between devices, on_device(): lax.psum((attn_gain_grad, query_w_grad, key_w_grad, value_w_grad, out_w_g...  175 us
    psum x1, blocking collectives, on_device(): lax.psum((attn_gain_grad, query_w_grad, key_w_grad, value_w_grad, out_w_g...  108 us
    ppermute x15, starting transfers between devices, _proceed_stages_all(): lax.ppermute(seen_now, axis_name=ax_name, perm=[(i0, i0 ^ jj) for i0 in r...  79.1 us
    all_to_all x1, starting transfers between devices, on_device(): lax.all_to_all(outputs.reshape(experts, slot_count, model_width), 'wide',...  70.4 us
  transfers between devices with their start and end apart: 25, of which 12 were waited for; matrix products, arithmetic and copies ran while one was open for 18% of the time, Pallas kernels for 0%

profile of v1, /device:TPU:0, one launch (start us, length us, event | category | flops | bytes accessed | tf_op | source)
XLA Modules:
  0.0 2214.8 jit_solution(3742878294250864853)
XLA Ops:
  17.6 16.1 scatter_custom_fusion
  70.6 35.4 %gather_fusion = bf16[8192,1024]{1,0:T(8,128)(2,1)} fusion(bf16[513,1024]{1,0:T(8,128)(2,1)S(1)} %concatenate.31, s32[8192]{0:T(1024)S(1)} %fusion.53), kind=kCustom, calls=%fused_computation | custom fusion | bytes 33587200 | tf_op jit(solution)/shard_map/gather | solution.py:142
  115.7 22.7 %all-gather.4.cloned.1.call-done = bf16[1,1024,512]{2,1,0:T(8,128)(2,1)} async-done(((bf16[1,1024,256]{2,1,0:T(8,128)(2,1)}), bf16[1,1024,512]{2,1,0:T(8,128)(2,1)}) %all-gather.4.cloned.1.call-update) | async-done | bytes 1048592 | tf_op jit(solution)/shard_map/all_gather | solution.py:146
  138.4 271.7 %all-to-all-done = bf16[16,512,1024]{2,1,0:T(8,128)(2,1)} async-done(((bf16[16,512,1024]{2,1,0:T(8,128)(2,1)}), bf16[16,512,1024]{2,1,0:T(8,128)(2,1)}, u32[]{:S(2)}, u32[]{:S(2)}) %all-to-all-start) | async-done | bytes 16777248 | tf_op jit(solution)/shard_map/all_to_all | solution.py:143
  410.1 15.9 fusion.44
  426.1 21.8 multiply_convert_fusion.2
  447.9 15.0 convolution_convert_fusion
  463.0 70.4 %all-to-all-start.1 = ((bf16[16,512,1024]{2,1,0:T(8,128)(2,1)}), bf16[16,512,1024]{2,1,0:T(8,128)(2,1)}, u32[]{:S(2)}, u32[]{:S(2)}) async-start(bf16[16,512,1024]{2,1,0:T(8,128)(2,1)} %bitcast.237), calls=%async_computation.1 | async-start | bytes 33554432 | tf_op jit(solution)/shard_map/all_to_all | solution.py:154
  535.0 35.4 %gather_fusion.2 = bf16[8192,1024]{1,0:T(8,128)(2,1)} fusion(bf16[513,1024]{1,0:T(8,128)(2,1)S(1)} %concatenate.32, s32[8192]{0:T(1024)S(1)} %fusion.53), kind=kCustom, calls=%fused_computation.2 | custom fusion | bytes 33587200 | tf_op jit(solution)/shard_map/gather | solution.py:174
  572.0 33.0 %gather_fusion.5 = f32[4096]{0:T(1024)S(1)} fusion(f32[512,16]{0,1:T(8,128)S(1)} %fusion.83, s32[4096]{0:T(1024)S(1)} %reshape.361), kind=kCustom, calls=%fused_computation.5 | custom fusion | bytes 65536 | tf_op jit(solution)/shard_map/jit(take_along_axis)/gather | solution.py:130
  605.5 224.6 %all-to-all-done.1 = bf16[16,512,1024]{2,1,0:T(8,128)(2,1)} async-done(((bf16[16,512,1024]{2,1,0:T(8,128)(2,1)}), bf16[16,512,1024]{2,1,0:T(8,128)(2,1)}, u32[]{:S(2)}, u32[]{:S(2)}) %all-to-all-start.1) | async-done | bytes 16777248 | tf_op jit(solution)/shard_map/all_to_all | solution.py:154
  830.0 28.8 %gather_fusion.1 = bf16[4096,1024]{1,0:T(8,128)(2,1)} fusion(bf16[8192,1024]{1,0:T(8,128)(2,1)} %bitcast.23, s32[4096]{0:T(1024)S(1)} %broadcast_clamp_fusion), kind=kCustom, calls=%fused_computation.1 | custom fusion | bytes 16793600 | tf_op jit(solution)/shard_map/gather | solution.py:161
  867.2 15.5 scatter_custom_fusion.1
  882.8 14.7 fusion
  897.5 70.4 %all-to-all-start.2 = ((bf16[16,512,1024]{2,1,0:T(8,128)(2,1)}), bf16[16,512,1024]{2,1,0:T(8,128)(2,1)}, u32[]{:S(2)}, u32[]{:S(2)}) async-start(bf16[16,512,1024]{2,1,0:T(8,128)(2,1)} %fusion), calls=%async_computation.2 | async-start | bytes 33554432 | tf_op jit(solution)/shard_map/all_to_all | solution.py:175
  979.9 284.7 %all-to-all-done.2 = bf16[16,512,1024]{2,1,0:T(8,128)(2,1)} async-done(((bf16[16,512,1024]{2,1,0:T(8,128)(2,1)}), bf16[16,512,1024]{2,1,0:T(8,128)(2,1)}, u32[]{:S(2)}, u32[]{:S(2)}) %all-to-all-start.2) | async-done | bytes 16777248 | tf_op jit(solution)/shard_map/all_to_all | solution.py:175
  1264.6 15.7 fusion.27
  1280.6 28.7 %multiply_convert_fusion = (bf16[8192,512]{1,0:T(8,128)(2,1)}, bf16[8192,512]{1,0:T(8,128)(2,1)}) fusion(f32[8192,512]{1,0:T(8,128)} %fusion.44, f32[8192,512]{1,0:T(8,128)} %get-tuple-element.65, bf16[8192,1024]{1,0:T(8,128)(2,1)} %bitcast.28, bf16[1,512,1024]{2,1,0:T(8,128)(2,1)} %all-gather.8.cloned.1.call-done), kind=kOutput, calls=%fused_computation.18 | convolution fusion | flops 8644460544 | bytes 68157440 | tf_op jit(solution)/shard_map/rd,fd->rf/dot_general | solution.py:183
  1309.2 18.8 fusion.42
  1328.0 23.6 %add_convert_fusion = bf16[8192,1024]{1,0:T(8,128)(2,1)} fusion(f32[8192,1024]{1,0:T(8,128)} %fusion.42, bf16[8192,512]{1,0:T(8,128)(2,1)} %get-tuple-element.25, bf16[1,1024,512]{2,1,0:T(8,128)(2,1)} %all-gather.6.cloned.1.call-done), kind=kOutput, calls=%fused_computation.10 | convolution fusion | flops 8606711808 | bytes 59768832 | tf_op jit(solution)/shard_map/rf,df->rd/dot_general | solution.py:194
  1364.2 65.7 %collective-permute-start.3 = (bf16[1,512,1024]{2,1,0:T(8,128)(2,1)}, bf16[1,512,1024]{2,1,0:T(8,128)(2,1)}, u32[]{:S(2)}, u32[]{:S(2)}) collective-permute-start(bf16[1,512,1024]{2,1,0:T(8,128)(2,1)} %get-tuple-element.38), channel_id=1, source_target_pairs={{0,8},{2,10},{4,12},{6,14},{8,0},{10,2},{12,4},{14,6},{16,24},{18,... | collective-permute-start | bytes 3145736 | tf_op jit(solution)/shard_map/ppermute | solution.py:28
  1446.3 15.7 fusion.25
  1468.0 33.7 %collective-permute-done.1 = bf16[1,512,1024]{2,1,0:T(8,128)(2,1)} collective-permute-done((bf16[1,512,1024]{2,1,0:T(8,128)(2,1)}, bf16[1,512,1024]{2,1,0:T(8,128)(2,1)}, u32[]{:S(2)}, u32[]{:S(2)}) %collective-permute-start.1) | collective-permute-done | bytes 1048608 | tf_op jit(solution)/shard_map/ppermute | solution.py:28
  1511.4 24.1 %collective-permute-done.4 = bf16[1,512,1024]{2,1,0:T(8,128)(2,1)S(1)} collective-permute-done((bf16[1,512,1024]{2,1,0:T(8,128)(2,1)}, bf16[1,512,1024]{2,1,0:T(8,128)(2,1)S(1)}, u32[]{:S(2)}, u32[]{:S(2)}) %collective-permute-start.4) | collective-permute-done | bytes 1048608 | tf_op jit(solution)/shard_map/ppermute | solution.py:28
  1536.6 42.3 %collective-permute-done.5 = bf16[1,512,1024]{2,1,0:T(8,128)(2,1)S(1)} collective-permute-done((bf16[1,512,1024]{2,1,0:T(8,128)(2,1)}, bf16[1,512,1024]{2,1,0:T(8,128)(2,1)S(1)}, u32[]{:S(2)}, u32[]{:S(2)}) %collective-permute-start.5) | collective-permute-done | bytes 1048608 | tf_op jit(solution)/shard_map/ppermute | solution.py:28
  1579.9 21.3 collective-permute-done.6
  1605.1 68.8 %collective-permute-done.8 = bf16[1,512,1024]{2,1,0:T(8,128)(2,1)S(1)} collective-permute-done((bf16[1,512,1024]{2,1,0:T(8,128)(2,1)S(1)}, bf16[1,512,1024]{2,1,0:T(8,128)(2,1)S(1)}, u32[]{:S(2)}, u32[]{:S(2)}) %collective-permute-start.8) | collective-permute-done | bytes 1048608 | tf_op jit(solution)/shard_map/ppermute | solution.py:28
  1675.0 41.3 %collective-permute-done.9 = bf16[1,512,1024]{2,1,0:T(8,128)(2,1)S(1)} collective-permute-done((bf16[1,512,1024]{2,1,0:T(8,128)(2,1)S(1)}, bf16[1,512,1024]{2,1,0:T(8,128)(2,1)S(1)}, u32[]{:S(2)}, u32[]{:S(2)}) %collective-permute-start.9) | collective-permute-done | bytes 1048608 | tf_op jit(solution)/shard_map/ppermute | solution.py:28
  1719.8 41.7 %collective-permute-done.10 = bf16[1,512,1024]{2,1,0:T(8,128)(2,1)S(1)} collective-permute-done((bf16[1,512,1024]{2,1,0:T(8,128)(2,1)S(1)}, bf16[1,512,1024]{2,1,0:T(8,128)(2,1)S(1)}, u32[]{:S(2)}, u32[]{:S(2)}) %collective-permute-start.10) | collective-permute-done | bytes 1048608 | tf_op jit(solution)/shard_map/ppermute | solution.py:28
  1781.1 29.0 %gather_fusion.4 = bf16[4096,1024]{1,0:T(8,128)(2,1)} fusion(bf16[8192,1024]{1,0:T(8,128)(2,1)} %bitcast.232, s32[4096]{0:T(1024)S(1)} %copy-done.43), kind=kCustom, calls=%fused_computation.4 | custom fusion | bytes 16793600 | tf_op jit(solution)/shard_map/gather | solution.py:210
  1904.3 107.7 %all-reduce.2 = (f32[1024]{0:T(1024)}, f32[1024]{0:T(1024)}) all-reduce(f32[1024]{0:T(1024)S(1)} %get-tuple-element.14, f32[1024]{0:T(1024)S(1)} %get-tuple-element.12), channel_id=1, replica_groups=mesh['wide'=16,'narrow'=2] {'wide','narrow'}, use_global_device_ids=true, to_apply=%region_20.21 | all-reduce | flops 2048 | bytes 16384 | tf_op jit(solution)/shard_map/psum | solution.py:253
  2022.2 175.1 %all-reduce.6.cloned.1.call-done = (f32[1024,1024]{1,0:T(8,128)}, f32[1024,512]{1,0:T(8,128)}, f32[1024,512]{1,0:T(8,128)}, f32[1024,1024]{1,0:T(8,128)}, f32[1024,16]{0,1:T(8,128)}) async-done(((f32[1024,1024]{1,0:T(8,128)}, f32[1024,512]{1,0:T(8,128)}, f32[1024,512]{1,0:T(8,128)}, f32[1024,1024]{1,0:T(8,128)}, f32[1024,16]{0,1:T(8,128)}), (f32[1024,1024]{1,0:T(8,128)}, f32[1024,512]{1,0:T(8,128)}, ...) | async-done | bytes 12648464 | tf_op jit(solution)/shard_map/psum | solution.py:253
  (276 shorter events, 269.7 us)
Async XLA Ops:
  106.0 304.1 %all-to-all-start = ((bf16[16,512,1024]{2,1,0:T(8,128)(2,1)}), bf16[16,512,1024]{2,1,0:T(8,128)(2,1)}, u32[]{:S(2)}, u32[]{:S(2)}) async-start(bf16[16,512,1024]{2,1,0:T(8,128)(2,1)} %bitcast.234), calls=%async_computation | async-start | bytes 33554432 | tf_op jit(solution)/shard_map/all_to_all | solution.py:143
  113.5 24.9 %all-gather.4.cloned.1.call-start = ((), (), s32[]{:S(2)}) async-start(), calls=%async_computation.6 | async-start | bytes 1572864 | tf_op jit(solution)/shard_map/all_gather | solution.py:146
  114.3 311.8 %all-gather.6.cloned.1.call-start = ((), (), s32[]{:S(2)}) async-start(), calls=%async_computation.7 | async-start | bytes 1572864 | tf_op jit(solution)/shard_map/all_gather | solution.py:147
  115.0 332.9 %all-gather.8.cloned.1.call-start = ((), (), s32[]{:S(2)}) async-start(), calls=%async_computation.8 | async-start | bytes 1572864 | tf_op jit(solution)/shard_map/all_gather | solution.py:148
  463.0 367.0 %all-to-all-start.1 = ((bf16[16,512,1024]{2,1,0:T(8,128)(2,1)}), bf16[16,512,1024]{2,1,0:T(8,128)(2,1)}, u32[]{:S(2)}, u32[]{:S(2)}) async-start(bf16[16,512,1024]{2,1,0:T(8,128)(2,1)} %bitcast.237), calls=%async_computation.1 | async-start | bytes 33554432 | tf_op jit(solution)/shard_map/all_to_all | solution.py:154
  605.4 253.4 %copy-start.42 = (s32[4096]{0:T(1024)}, s32[4096]{0:T(1024)S(1)}, u32[]{:S(2)}) copy-start(s32[4096]{0:T(1024)S(1)} %broadcast_clamp_fusion) | copy-start | bytes 49156
  897.5 367.0 %all-to-all-start.2 = ((bf16[16,512,1024]{2,1,0:T(8,128)(2,1)}), bf16[16,512,1024]{2,1,0:T(8,128)(2,1)}, u32[]{:S(2)}, u32[]{:S(2)}) async-start(bf16[16,512,1024]{2,1,0:T(8,128)(2,1)} %fusion), calls=%async_computation.2 | async-start | bytes 33554432 | tf_op jit(solution)/shard_map/all_to_all | solution.py:175
  967.9 1048.0 %reduce-scatter.8.cloned.1.call-start = ((), (), s32[]{:S(2)}) async-start(), calls=%async_computation.11 | async-start | bytes 1572864 | tf_op jit(solution)/shard_map/reduce_scatter | solution.py:203
  1280.3 737.7 %reduce-scatter.6.cloned.1.call-start = ((), (), s32[]{:S(2)}) async-start(), calls=%async_computation.10 | async-start | bytes 1572864 | tf_op jit(solution)/shard_map/reduce_scatter | solution.py:200
  1364.2 143.9 %collective-permute-start.3 = (bf16[1,512,1024]{2,1,0:T(8,128)(2,1)}, bf16[1,512,1024]{2,1,0:T(8,128)(2,1)}, u32[]{:S(2)}, u32[]{:S(2)}) collective-permute-start(bf16[1,512,1024]{2,1,0:T(8,128)(2,1)} %get-tuple-element.38), channel_id=1, source_target_pairs={{0,8},{2,10},{4,12},{6,14},{8,0},{10,2},{12,4},{14,6},{16,24},{18,... | collective-permute-start | bytes 3145736 | tf_op jit(solution)/shard_map/ppermute | solution.py:28
  1429.9 74.1 %collective-permute-start.2 = (bf16[1,512,1024]{2,1,0:T(8,128)(2,1)}, bf16[1,512,1024]{2,1,0:T(8,128)(2,1)}, u32[]{:S(2)}, u32[]{:S(2)}) collective-permute-start(bf16[1,512,1024]{2,1,0:T(8,128)(2,1)} %get-tuple-element.39), channel_id=1, source_target_pairs={{0,6},{2,4},{4,2},{6,0},{8,14},{10,12},{12,10},{14,8},{16,22},{18,... | collective-permute-start | bytes 3145736 | tf_op jit(solution)/shard_map/ppermute | solution.py:28
  1432.7 69.0 %collective-permute-start.1 = (bf16[1,512,1024]{2,1,0:T(8,128)(2,1)}, bf16[1,512,1024]{2,1,0:T(8,128)(2,1)}, u32[]{:S(2)}, u32[]{:S(2)}) collective-permute-start(bf16[1,512,1024]{2,1,0:T(8,128)(2,1)} %get-tuple-element.40), channel_id=1, source_target_pairs={{0,4},{2,6},{4,0},{6,2},{8,12},{10,14},{12,8},{14,10},{16,20},{18,... | collective-permute-start | bytes 3145736 | tf_op jit(solution)/shard_map/ppermute | solution.py:28
  1432.9 32.6 %collective-permute-start = (bf16[1,512,1024]{2,1,0:T(8,128)(2,1)}, bf16[1,512,1024]{2,1,0:T(8,128)(2,1)}, u32[]{:S(2)}, u32[]{:S(2)}) collective-permute-start(bf16[1,512,1024]{2,1,0:T(8,128)(2,1)} %get-tuple-element.41), channel_id=1, source_target_pairs={{0,2},{2,0},{4,6},{6,4},{8,10},{10,8},{12,14},{14,12},{16,18},{18,... | collective-permute-start | bytes 3145736 | tf_op jit(solution)/shard_map/ppermute | solution.py:28
  1446.3 573.9 %reduce-scatter.4.cloned.1.call-start = ((), (), s32[]{:S(2)}) async-start(), calls=%async_computation.9 | async-start | bytes 1572864 | tf_op jit(solution)/shard_map/reduce_scatter | solution.py:197
  1462.0 303.8 %collective-permute-start.14 = (bf16[1,512,1024]{2,1,0:T(8,128)(2,1)S(1)}, bf16[1,512,1024]{2,1,0:T(8,128)(2,1)}, u32[]{:S(2)}, u32[]{:S(2)}) collective-permute-start(bf16[1,512,1024]{2,1,0:T(8,128)(2,1)S(1)} %get-tuple-element.27), channel_id=1, source_target_pairs={{0,30},{2,28},{4,26},{6,24},{8,22},{10,20},{12,18},{14,16},{16,14}... | collective-permute-start | bytes 3145736 | tf_op jit(solution)/shard_map/ppermute | solution.py:28
  1465.4 732.0 %all-reduce.6.cloned.1.call-start = ((), (), s32[]{:S(2)}) async-start(), calls=%async_computation.12 | async-start | bytes 25296896 | tf_op jit(solution)/shard_map/psum | solution.py:253
  1465.4 113.4 %copy-start.30 = (bf16[1,512,1024]{2,1,0:T(8,128)(2,1)S(1)}, bf16[1,512,1024]{2,1,0:T(8,128)(2,1)}, u32[]{:S(2)}) copy-start(bf16[1,512,1024]{2,1,0:T(8,128)(2,1)} %get-tuple-element.32) | copy-start | bytes 3145732
  1465.5 135.8 %copy-start.29 = (bf16[1,512,1024]{2,1,0:T(8,128)(2,1)S(1)}, bf16[1,512,1024]{2,1,0:T(8,128)(2,1)}, u32[]{:S(2)}) copy-start(bf16[1,512,1024]{2,1,0:T(8,128)(2,1)} %get-tuple-element.31) | copy-start | bytes 3145732
  1465.5 136.9 %copy-start.28 = (bf16[1,512,1024]{2,1,0:T(8,128)(2,1)S(1)}, bf16[1,512,1024]{2,1,0:T(8,128)(2,1)}, u32[]{:S(2)}) copy-start(bf16[1,512,1024]{2,1,0:T(8,128)(2,1)} %get-tuple-element.30) | copy-start | bytes 3145732
  1465.5 70.0 %collective-permute-start.4 = (bf16[1,512,1024]{2,1,0:T(8,128)(2,1)}, bf16[1,512,1024]{2,1,0:T(8,128)(2,1)S(1)}, u32[]{:S(2)}, u32[]{:S(2)}) collective-permute-start(bf16[1,512,1024]{2,1,0:T(8,128)(2,1)} %get-tuple-element.37), channel_id=1, source_target_pairs={{0,10},{2,8},{4,14},{6,12},{8,2},{10,0},{12,6},{14,4},{16,26},{18,... | collective-permute-start | bytes 3145736 | tf_op jit(solution)/shard_map/ppermute | solution.py:28
  1465.6 208.4 %copy-start.27 = (bf16[1,512,1024]{2,1,0:T(8,128)(2,1)S(1)}, bf16[1,512,1024]{2,1,0:T(8,128)(2,1)}, u32[]{:S(2)}) copy-start(bf16[1,512,1024]{2,1,0:T(8,128)(2,1)} %get-tuple-element.29) | copy-start | bytes 3145732
  1501.7 214.6 %copy-start.26 = (bf16[1,512,1024]{2,1,0:T(8,128)(2,1)S(1)}, bf16[1,512,1024]{2,1,0:T(8,128)(2,1)}, u32[]{:S(2)}) copy-start(bf16[1,512,1024]{2,1,0:T(8,128)(2,1)} %get-tuple-element.28) | copy-start | bytes 3145732
  1501.7 77.2 %collective-permute-start.5 = (bf16[1,512,1024]{2,1,0:T(8,128)(2,1)}, bf16[1,512,1024]{2,1,0:T(8,128)(2,1)S(1)}, u32[]{:S(2)}, u32[]{:S(2)}) collective-permute-start(bf16[1,512,1024]{2,1,0:T(8,128)(2,1)} %get-tuple-element.36), channel_id=1, source_target_pairs={{0,12},{2,14},{4,8},{6,10},{8,4},{10,6},{12,0},{14,2},{16,28},{18,... | collective-permute-start | bytes 3145736 | tf_op jit(solution)/shard_map/ppermute | solution.py:28
  1504.0 97.2 %collective-permute-start.6 = (bf16[1,512,1024]{2,1,0:T(8,128)(2,1)}, bf16[1,512,1024]{2,1,0:T(8,128)(2,1)S(1)}, u32[]{:S(2)}, u32[]{:S(2)}) collective-permute-start(bf16[1,512,1024]{2,1,0:T(8,128)(2,1)} %get-tuple-element.35), channel_id=1, source_target_pairs={{0,14},{2,12},{4,10},{6,8},{8,6},{10,4},{12,2},{14,0},{16,30},{18,... | collective-permute-start | bytes 3145736 | tf_op jit(solution)/shard_map/ppermute | solution.py:28
  1508.2 94.2 %collective-permute-start.7 = (bf16[1,512,1024]{2,1,0:T(8,128)(2,1)}, bf16[1,512,1024]{2,1,0:T(8,128)(2,1)S(1)}, u32[]{:S(2)}, u32[]{:S(2)}) collective-permute-start(bf16[1,512,1024]{2,1,0:T(8,128)(2,1)} %get-tuple-element.34), channel_id=1, source_target_pairs={{0,16},{2,18},{4,20},{6,22},{8,24},{10,26},{12,28},{14,30},{16,0},... | collective-permute-start | bytes 3145736 | tf_op jit(solution)/shard_map/ppermute | solution.py:28
  1535.5 138.4 %collective-permute-start.8 = (bf16[1,512,1024]{2,1,0:T(8,128)(2,1)S(1)}, bf16[1,512,1024]{2,1,0:T(8,128)(2,1)S(1)}, u32[]{:S(2)}, u32[]{:S(2)}) collective-permute-start(bf16[1,512,1024]{2,1,0:T(8,128)(2,1)S(1)} %copy-done.31), channel_id=1, source_target_pairs={{0,18},{2,16},{4,22},{6,20},{8,26},{10,24},{12,30},{14,28},{16,2},... | collective-permute-start | bytes 3145736 | tf_op jit(solution)/shard_map/ppermute | solution.py:28
  1578.9 137.4 %collective-permute-start.9 = (bf16[1,512,1024]{2,1,0:T(8,128)(2,1)S(1)}, bf16[1,512,1024]{2,1,0:T(8,128)(2,1)S(1)}, u32[]{:S(2)}, u32[]{:S(2)}) collective-permute-start(bf16[1,512,1024]{2,1,0:T(8,128)(2,1)S(1)} %copy-done.30), channel_id=1, source_target_pairs={{0,20},{2,22},{4,16},{6,18},{8,28},{10,30},{12,24},{14,26},{16,4},... | collective-permute-start | bytes 3145736 | tf_op jit(solution)/shard_map/ppermute | solution.py:28
  1601.2 160.3 %collective-permute-start.10 = (bf16[1,512,1024]{2,1,0:T(8,128)(2,1)S(1)}, bf16[1,512,1024]{2,1,0:T(8,128)(2,1)S(1)}, u32[]{:S(2)}, u32[]{:S(2)}) collective-permute-start(bf16[1,512,1024]{2,1,0:T(8,128)(2,1)S(1)} %copy-done.29), channel_id=1, source_target_pairs={{0,22},{2,20},{4,18},{6,16},{8,30},{10,28},{12,26},{14,24},{16,6},... | collective-permute-start | bytes 3145736 | tf_op jit(solution)/shard_map/ppermute | solution.py:28
  1602.3 160.3 %collective-permute-start.11 = (bf16[1,512,1024]{2,1,0:T(8,128)(2,1)S(1)}, bf16[1,512,1024]{2,1,0:T(8,128)(2,1)S(1)}, u32[]{:S(2)}, u32[]{:S(2)}) collective-permute-start(bf16[1,512,1024]{2,1,0:T(8,128)(2,1)S(1)} %copy-done.28), channel_id=1, source_target_pairs={{0,24},{2,26},{4,28},{6,30},{8,16},{10,18},{12,20},{14,22},{16,8},... | collective-permute-start | bytes 3145736 | tf_op jit(solution)/shard_map/ppermute | solution.py:28
  1673.9 89.7 %collective-permute-start.12 = (bf16[1,512,1024]{2,1,0:T(8,128)(2,1)S(1)}, bf16[1,512,1024]{2,1,0:T(8,128)(2,1)S(1)}, u32[]{:S(2)}, u32[]{:S(2)}) collective-permute-start(bf16[1,512,1024]{2,1,0:T(8,128)(2,1)S(1)} %copy-done.27), channel_id=1, source_target_pairs={{0,26},{2,24},{4,30},{6,28},{8,18},{10,16},{12,22},{14,20},{16,10}... | collective-permute-start | bytes 3145736 | tf_op jit(solution)/shard_map/ppermute | solution.py:28
  1716.3 48.4 %collective-permute-start.13 = (bf16[1,512,1024]{2,1,0:T(8,128)(2,1)S(1)}, bf16[1,512,1024]{2,1,0:T(8,128)(2,1)S(1)}, u32[]{:S(2)}, u32[]{:S(2)}) collective-permute-start(bf16[1,512,1024]{2,1,0:T(8,128)(2,1)S(1)} %copy-done.26), channel_id=1, source_target_pairs={{0,28},{2,30},{4,24},{6,26},{8,20},{10,22},{12,16},{14,18},{16,12}... | collective-permute-start | bytes 3145736 | tf_op jit(solution)/shard_map/ppermute | solution.py:28
  1898.5 113.5 %copy-start.56 = (f32[512]{0:T(512)S(1)}, f32[512]{0:T(512)}, u32[]{:S(2)}) copy-start(f32[512]{0:T(512)} %get-tuple-element.53) | copy-start | bytes 6148
  (57 other events, 958.2 us)
Sparse Core Ops, SparseCore 0:
  115.9 22.5 all-gather.3
  139.9 21.2 all-gather.5
  162.8 21.2 all-gather.7
  1280.4 85.9 reduce-scatter.7
  1446.4 20.6 reduce-scatter.5
  1469.2 20.3 reduce-scatter.3
  1896.3 301.0 all-reduce.5
